TPU v7x, 32 devices: a 4x2x2 block of a 4x4x8 slice. The times are simulated.
32 devices in a mesh: data: 4 (over y, z), seq: 8 (over x, core).
Axes of the slice: x: 4, y: 2, z: 2, core: 2. Of those that a mesh axis runs over, the one named last changes fastest.
The devices are a block of a 4x4x8 slice.
Arguments:
- act_in: bfloat16 [16, 2048, 1280], P('data', 'seq'), parts along dimension 0
- ln1_scale: float32 [1280], replicated
- ln1_bias: float32 [1280], replicated
- w_in: bfloat16 [1280, 5120], replicated
- b_in: float32 [5120], replicated
- ln2_scale: float32 [2560], replicated
- ln2_bias: float32 [2560], replicated
- w_spatial: bfloat16 [2048, 2048], replicated
- b_spatial: float32 [2048], replicated
- causal_mask: int32 [2048, 2048], replicated
- w_out: bfloat16 [2560, 1280], replicated
- b_out: float32 [1280], replicated
Outputs:
- output: bfloat16 [16, 2048, 1280], P('data', 'seq'), parts along dimension 0
There are 4 independent parts. A program takes and returns all parts, laid end to end along the dimension named above; an argument that names none is the same for every part.
All inputs are finite; a program needn't handle non-finite values.
Results may differ from a plain program's by a relative error of at most 0.011577.
Values are sent between devices in bfloat16 or wider.
A program may use at most 768 MiB of HBM per device.

v0:
```python
import jax
import jax.numpy as jnp
from jax import lax
from jax.sharding import PartitionSpec as P

LN_EPS = 1e-6


def layer_norm(features, ln_gain, ln_shift):
    mean_val = jnp.mean(features, axis=-1, keepdims=True)
    centered = features - mean_val
    var_val = jnp.mean(centered * centered, axis=-1, keepdims=True)
    return centered * lax.rsqrt(var_val + LN_EPS) * ln_gain + ln_shift


def solution(mesh):
    row_spec = P('data', 'seq', None)
    replicated = P()

    def local_block(act_in, ln1_scale, ln1_bias, w_in, b_in, ln2_scale, ln2_bias, w_spatial, b_spatial, causal_mask, w_out, b_out):
        gate_dim = w_out.shape[0]
        normed = layer_norm(act_in.astype(jnp.float32), ln1_scale, ln1_bias).astype(jnp.bfloat16)
        hidden = jax.nn.gelu(jnp.einsum('bsd,df->bsf', normed, w_in, preferred_element_type=jnp.float32) + b_in, approximate=True).astype(jnp.bfloat16)
        gate_half = hidden[:, :, :gate_dim]
        value_norm = layer_norm(hidden[:, :, gate_dim:].astype(jnp.float32), ln2_scale, ln2_bias).astype(jnp.bfloat16)
        value_cols = lax.all_to_all(value_norm, 'seq', 2, 1, tiled=True)
        w_masked = jnp.where(causal_mask > 0, w_spatial, jnp.zeros_like(w_spatial))
        spatial_cols = (jnp.einsum('ij,bjc->bic', w_masked, value_cols, preferred_element_type=jnp.float32) + b_spatial[None, :, None]).astype(jnp.bfloat16)
        spatial_rows = lax.all_to_all(spatial_cols, 'seq', 1, 2, tiled=True)
        gated_act = (gate_half.astype(jnp.float32) * spatial_rows.astype(jnp.float32)).astype(jnp.bfloat16)
        projected = jnp.einsum('bsc,cd->bsd', gated_act, w_out, preferred_element_type=jnp.float32) + b_out
        return (act_in.astype(jnp.float32) + projected).astype(jnp.bfloat16)

    return jax.shard_map(local_block, mesh=mesh, in_specs=(row_spec,) + (replicated,) * 11, out_specs=row_spec, check_vma=False)
```

profile of v0, /device:TPU:81, one launch (start us, length us, event | category | flops | bytes accessed | tf_op | source)
XLA Modules:
  0.0 275.6 jit_solution(784447670484368527)
XLA Ops:
  0.0 2.2 convert_reduce_fusion.1
  2.2 2.6 fusion.26
  4.8 21.3 %fusion.7 = bf16[4,256,5120]{2,1,0:T(8,128)(2,1)S(1)} fusion(f32[5120]{0:T(1024)} %param.16, bf16[1280,5120]{1,0:T(8,128)(2,1)} %param.15, bf16[4,256,1280]{2,1,0:T(8,128)(2,1)} %param.12, f32[1280]{0:T(1024)} %param.14, f32[1280]{0:T(1024)} %param.13, f32[4,256]{1,0:T(4,128)S(1)} %add_rsqrt_fusion.1, f32[4,256]{1,0:T(4,128)S(1)} %broadcast_multiply_fusion.1), kind=kOutput, calls=%fused_computation.8 | convolution fusion | flops 13482065920 | bytes 26253312 | tf_op jit(solution)/shard_map/bsd,df->bsf/dot_general | solution.py:23
  26.1 0.0 copy-start
  26.1 0.0 copy-start.2
  26.1 0.0 copy-start.3
  26.1 0.8 convert_reduce_fusion
  26.9 1.5 fusion.12
  28.4 1.7 copy-done
  30.1 0.0 copy-done.2
  30.1 0.0 copy-done.3
  30.1 4.0 %fusion.15 = bf16[4,256,2560]{2,1,0:T(8,128)(2,1)} fusion(f32[2560]{0:T(1024)S(1)} %copy-done.2, f32[2560]{0:T(1024)S(1)} %copy-done.3, f32[4,256]{1,0:T(4,128)S(1)} %add_rsqrt_fusion, f32[4,256]{1,0:T(4,128)S(1)} %broadcast_multiply_fusion, bf16[4,256,5120]{2,1,0:T(8,128)(2,1)S(1)} %fusion.7), kind=kLoop, calls=%fused_computation.19 | loop fusion | flops 15728640 | bytes 10514432 | tf_op jit(solution)/shard_map/convert_element_type | solution.py:25
  34.1 9.0 %copy.31 = bf16[4,256,2560]{1,0,2:T(4,128)(2,1)} copy(bf16[4,256,2560]{2,1,0:T(8,128)(2,1)} %fusion.15) | data formatting | bytes 10485760 | tf_op jit(solution)/shard_map/convert_element_type | solution.py:25
  43.1 65.9 %all_to_all.27 = bf16[4,256,2560]{1,0,2:T(4,128)(2,1)S(1)} all-to-all(bf16[4,256,2560]{1,0,2:T(4,128)(2,1)} %copy.31), channel_id=1, replica_groups=mesh['data'=4,'seq'=8] {'seq'}, dimensions={2} | all-to-all | bytes 10485760 | tf_op jit(solution)/shard_map/all_to_all | solution.py:26
  109.0 0.0 copy-start.4
  109.0 0.7 copy.32
  109.7 0.7 copy.38
  110.4 0.0 copy-done.4
  110.4 17.7 %fusion.31 = bf16[4,2048,320]{1,2,0:T(8,128)(2,1)} fusion(f32[2048]{0:T(1024)S(1)} %copy-done.4, bf16[4,2048,320]{1,2,0:T(8,128)(2,1)S(1)} %bitcast.36, bf16[2048,2048]{1,0:T(8,128)(2,1)} %param.19, s32[2048,2048]{1,0:T(8,128)} %param.21), kind=kOutput, calls=%fused_computation.37 | convolution fusion | flops 10751049728 | bytes 35659776 | tf_op jit(solution)/shard_map/ij,bjc->bic/dot_general | solution.py:28
  128.2 10.4 %copy.34 = bf16[4,2048,320]{2,0,1:T(4,128)(2,1)} copy(bf16[4,2048,320]{1,2,0:T(8,128)(2,1)} %fusion.31) | data formatting | bytes 10485760 | tf_op jit(solution)/shard_map/convert_element_type | solution.py:28
  138.5 77.3 %all_to_all.28 = bf16[4,2048,320]{2,0,1:T(4,128)(2,1)} all-to-all(bf16[4,2048,320]{2,0,1:T(4,128)(2,1)} %copy.34), channel_id=1, replica_groups=mesh['data'=4,'seq'=8] {'seq'}, dimensions={1} | all-to-all | bytes 10485760 | tf_op jit(solution)/shard_map/all_to_all | solution.py:29
  215.9 10.4 %copy.35 = bf16[4,2048,320]{1,2,0:T(8,128)(2,1)} copy(bf16[4,2048,320]{2,0,1:T(4,128)(2,1)} %all_to_all.28) | data formatting | bytes 10485760 | tf_op jit(solution)/shard_map/all_to_all | solution.py:29
  226.3 3.9 %convert_element_type.59 = f32[4,2048,320]{1,2,0:T(8,128)S(1)} convert(bf16[4,2048,320]{1,2,0:T(8,128)(2,1)} %copy.35) | non-fusion elementwise | flops 2621440 | bytes 15728640 | tf_op jit(solution)/shard_map/convert_element_type | solution.py:30
  230.2 9.2 %copy.39 = f32[160,8,8,256]{3,2,1,0:T(8,128)} copy(f32[160,8,8,256]{3,1,2,0:T(8,128)S(1)} %bitcast.32) | data formatting | bytes 20971520
  239.3 11.0 %copy.36 = f32[4,256,8,320]{1,3,2,0:T(8,128)} copy(f32[4,256,8,320]{1,2,3,0:T(8,128)} %bitcast.33) | data formatting | bytes 20971520 | tf_op jit(solution)/shard_map/convert_element_type | solution.py:30
  250.4 0.0 copy-start.1
  250.4 0.0 copy-start.5
  250.4 11.6 %copy.37 = f32[4,256,2560]{2,1,0:T(8,128)} copy(f32[4,256,2560]{1,2,0:T(8,128)} %bitcast.34) | data formatting | bytes 20971520 | tf_op jit(solution)/shard_map/convert_element_type | solution.py:30
  262.0 0.0 copy-done.1
  262.0 0.0 copy-done.5
  262.0 13.6 %fusion.30 = bf16[4,256,1280]{2,1,0:T(8,128)(2,1)} fusion(bf16[4,256,1280]{2,1,0:T(8,128)(2,1)S(1)} %copy-done.1, bf16[2560,1280]{1,0:T(8,128)(2,1)} %param.22, f32[4,256,2560]{2,1,0:T(8,128)} %copy.37, bf16[4,256,5120]{2,1,0:T(8,128)(2,1)} %copy-done, f32[1280]{0:T(1024)S(1)} %copy-done.5), kind=kOutput, calls=%fused_computation.36 | convolution fusion | flops 6723993600 | bytes 27530240 | tf_op jit(solution)/shard_map/bsc,cd->bsd/dot_general | solution.py:31
  (4 shorter events, 0.0 us)
Async XLA Ops:
  26.1 4.0 %copy-start = (bf16[4,256,5120]{2,1,0:T(8,128)(2,1)}, bf16[4,256,5120]{2,1,0:T(8,128)(2,1)S(1)}, u32[]{:S(2)}) copy-start(bf16[4,256,5120]{2,1,0:T(8,128)(2,1)S(1)} %fusion.7) | copy-start | bytes 31457284
  26.1 4.0 %copy-start.2 = (f32[2560]{0:T(1024)S(1)}, f32[2560]{0:T(1024)}, u32[]{:S(2)}) copy-start(f32[2560]{0:T(1024)} %param.18) | copy-start | bytes 30724
  26.1 4.0 %copy-start.3 = (f32[2560]{0:T(1024)S(1)}, f32[2560]{0:T(1024)}, u32[]{:S(2)}) copy-start(f32[2560]{0:T(1024)} %param.17) | copy-start | bytes 30724
  109.0 1.4 copy-start.4
  250.4 11.6 %copy-start.1 = (bf16[4,256,1280]{2,1,0:T(8,128)(2,1)S(1)}, bf16[4,256,1280]{2,1,0:T(8,128)(2,1)}, u32[]{:S(2)}) copy-start(bf16[4,256,1280]{2,1,0:T(8,128)(2,1)} %param.12) | copy-start | bytes 7864324
  250.4 11.6 %copy-start.5 = (f32[1280]{0:T(1024)S(1)}, f32[1280]{0:T(1024)}, u32[]{:S(2)}) copy-start(f32[1280]{0:T(1024)} %param.23) | copy-start | bytes 15364
where the time goes:
time: 277 us; the launch traced here: 276 us
  blocking collectives  143 us (52%)
  local copies, waits for them, and re-layouts  64.7 us (23%)
  matrix products  52.7 us (19%)
  other arithmetic  14.9 us (5%)
    all_to_all x1, blocking collectives, local_block(): spatial_rows = lax.all_to_all(spatial_cols, 'seq', 1, 2, tiled=True)  77.3 us
    all_to_all x1, blocking collectives, local_block(): value_cols = lax.all_to_all(value_norm, 'seq', 2, 1, tiled=True)  65.9 us
    convert_element_type x2, local copies, waits for them, and re-layouts, local_block(): spatial_rows.astype(jnp.float32)  22.6 us
    dot_general x1, matrix products, local_block(): jnp.einsum('bsd,df->bsf', normed, w_in, preferred_element_type=jnp.float32)  21.3 us
    dot_general x1, matrix products, local_block(): jnp.einsum('ij,bjc->bic', w_masked, value_cols, preferred_element_type=jn...  17.7 us
    dot_general x1, matrix products, local_block(): jnp.einsum('bsc,cd->bsd', gated_act, w_out, preferred_element_type=jnp.fl...  13.6 us
    unnamed x13, local copies, waits for them, and re-layouts  10.8 us
    all_to_all x1, local copies, waits for them, and re-layouts, local_block(): spatial_rows = lax.all_to_all(spatial_cols, 'seq', 1, 2, tiled=True)  10.4 us

commit v1 on v0

v1 whole, which is shorter than its diff:
```python
import functools

import jax
import jax.numpy as jnp
from jax import lax
from jax.experimental import pallas as pl
from jax.experimental.pallas import tpu as pltpu
from jax.sharding import PartitionSpec as P

LN_EPS = 1e-6
MESH = pl.DeviceIdType.MESH
GELU_A = 0.7978845608028654
GELU_B = 0.7978845608028654 * 0.044715
CORES = 2
NT = 512
OT = 256


def gelu(a):
    return (0.5 * a) * (1.0 + jnp.tanh(a * (GELU_A + GELU_B * (a * a))))


def block_kernel(chips, x_hbm, ln1s, ln1b, w_in_hbm, b_in, ln2s, ln2b, w_sp_hbm, b_sp, mask_hbm, w_out_hbm, b_out,
                 out_hbm,
                 w_in, w_out, xg, u, v, g, vn, wm, mk, q, o, bs,
                 w_in_sem, w_out_sem, wm_sem, mk_sem, own_sem, x_send, x_recv, v_send, v_recv, o_send, o_recv, o_loc):
    rows, model = x_hbm.shape[1:]
    gate = w_out.shape[0]
    n_in = gate // NT
    n_out = model // OT
    span = CORES * rows
    data = lax.axis_index("data")
    me = lax.axis_index("seq")
    chip = me // CORES
    core = me % CORES

    def device(c):
        return (data, c * CORES + core)

    partner = (data, chip * CORES + (1 - core))

    barrier = pltpu.get_barrier_semaphore()
    for d in range(1, chips):
        pl.semaphore_signal(barrier, inc=1, device_id=device((chip + d) % chips), device_id_type=MESH)
    pl.semaphore_signal(barrier, inc=1, device_id=partner, device_id_type=MESH)

    own_copy = pltpu.make_async_copy(x_hbm.at[chip], xg.at[chip], own_sem)
    own_copy.start()

    def w_in_copy(n):
        cols = pl.ds(pl.multiple_of(n * NT, NT), NT)
        return pltpu.make_async_copy(w_in_hbm.at[:, cols], w_in.at[:, cols], w_in_sem.at[n])

    for n in range(n_in):
        w_in_copy(n_in + n).start()

    pl.semaphore_wait(barrier, chips)

    def x_copy(d):
        to = (chip + d) % chips
        return pltpu.make_async_remote_copy(
            src_ref=x_hbm.at[to], dst_ref=xg.at[chip], send_sem=x_send.at[d], recv_sem=x_recv.at[d],
            device_id=device(to), device_id_type=MESH)

    for d in (2, 1, 3):
        x_copy(d).start()

    for n in range(n_in):
        w_in_copy(n).start()
    wm_copies, mk_copies = [], []
    t = 0
    for i in range(chips):
        r = pl.ds(pl.multiple_of((CORES * i + core) * rows, rows), rows)
        cp = pltpu.make_async_copy(w_sp_hbm.at[r, pl.ds(0, span * (i + 1))], wm.at[i, :, pl.ds(0, span * (i + 1))],
                                   wm_sem.at[i])
        cp.start()
        wm_copies.append(cp)
        for j in range(i + 1):
            cp = pltpu.make_async_copy(mask_hbm.at[r, pl.ds(span * j, span)], mk.at[t], mk_sem.at[t])
            cp.start()
            mk_copies.append(cp)
            t += 1
    w_out_copy = pltpu.make_async_copy(w_out_hbm, w_out, w_out_sem)
    w_out_copy.start()

    def hidden(k, j):
        own_rows = pl.multiple_of((CORES * j + core) * rows, rows)

        @pl.loop(0, rows // 32)
        def _(r):
            rr = pl.ds(pl.multiple_of(r * 32, 32), 32)
            xf = xg[j, rr, :].astype(jnp.float32)
            c = xf - jnp.mean(xf, axis=-1, keepdims=True)
            var = jnp.mean(c * c, axis=-1, keepdims=True)
            u[rr, :] = (c * lax.rsqrt(var + LN_EPS) * ln1s[...] + ln1b[...]).astype(jnp.bfloat16)

        @pl.loop(0, n_in)
        def _(n):
            @pl.when(k == 0)
            def _():
                w_in_copy(n_in + n).wait()

            cols = pl.ds(pl.multiple_of(n * NT, NT), NT)
            wcols = pl.ds(pl.multiple_of(gate + n * NT, NT), NT)
            a = jnp.dot(u[...], w_in[:, wcols], preferred_element_type=jnp.float32) + b_in[:, wcols]
            v[:, cols] = gelu(a).astype(jnp.bfloat16)

        @pl.loop(0, rows // 16)
        def _(r):
            rr = pl.ds(pl.multiple_of(r * 16, 16), 16)
            vf = v[rr, :].astype(jnp.float32)
            c = vf - jnp.mean(vf, axis=-1, keepdims=True)
            var = jnp.mean(c * c, axis=-1, keepdims=True)
            y = (c * lax.rsqrt(var + LN_EPS) * ln2s[...] + ln2b[...]).astype(jnp.bfloat16)
            vn[pl.ds(pl.multiple_of(own_rows + r * 16, 16), 16), :] = y

        @pl.loop(0, n_in)
        def _(n):
            @pl.when(k == 0)
            def _():
                w_in_copy(n).wait()

            cols = pl.ds(pl.multiple_of(n * NT, NT), NT)
            a = jnp.dot(u[...], w_in[:, cols], preferred_element_type=jnp.float32) + b_in[:, cols]
            g[j, :, cols] = gelu(a).astype(jnp.bfloat16)

            @pl.when(n == 0)
            def _():
                vn_copy(k, j).start()

    def vn_copy(k, j):
        r = pl.ds(pl.multiple_of((CORES * j + core) * rows, rows), rows)
        return pltpu.make_async_remote_copy(
            src_ref=vn.at[r], dst_ref=vn.at[r], send_sem=v_send.at[k], recv_sem=v_recv.at[k],
            device_id=partner, device_id_type=MESH)

    def mask_weights():
        for cp in wm_copies + mk_copies:
            cp.wait()
        t = 0
        for i in range(chips):
            for j in range(i + 1):
                cols = pl.ds(span * j, span)

                @pl.loop(0, rows // 32)
                def _(r, i=i, t=t, cols=cols):
                    rr = pl.ds(pl.multiple_of(r * 32, 32), 32)
                    w = wm[i, rr, cols].astype(jnp.float32)
                    wm[i, rr, cols] = jnp.where(mk[t, rr, :] > 0, w, 0.0).astype(jnp.bfloat16)

                t += 1
            row = b_sp[pl.ds(CORES * i + core, 1), :]
            bs[i, :, :] = jnp.transpose(jnp.broadcast_to(row, (128, rows)))

    def o_copy(i, n, recv):
        cols = pl.ds(pl.multiple_of(n * OT, OT), OT)
        return pltpu.make_async_remote_copy(
            src_ref=o.at[i, :, cols], dst_ref=out_hbm.at[chip, :, cols], send_sem=o_send.at[i, n],
            recv_sem=o_recv.at[recv, n], device_id=device(i), device_id_type=MESH)

    def o_local(n):
        cols = pl.ds(pl.multiple_of(n * OT, OT), OT)
        return pltpu.make_async_copy(o.at[chip, :, cols], out_hbm.at[chip, :, cols], o_loc.at[n])

    def mix(k, i):
        for s in range(chips):
            @pl.when(i == s)
            def _(s=s):
                depth = span * (s + 1)

                @pl.loop(0, n_in)
                def _(n):
                    cols = pl.ds(pl.multiple_of(n * NT, NT), NT)
                    acc = jnp.dot(wm[s, :, pl.ds(0, depth)], vn[pl.ds(0, depth), cols],
                                  preferred_element_type=jnp.float32)
                    sp = (acc + bs[s, :, 0:1]).astype(jnp.bfloat16).astype(jnp.float32)
                    q[:, cols] = (g[s, :, cols].astype(jnp.float32) * sp).astype(jnp.bfloat16)

        @pl.when(k == 1)
        def _():
            w_out_copy.wait()

        @pl.loop(0, n_out)
        def _(n):
            cols = pl.ds(pl.multiple_of(n * OT, OT), OT)
            y = jnp.dot(q[...], w_out[:, cols], preferred_element_type=jnp.float32) + b_out[:, cols]
            o[i, :, cols] = (xg[i, :, cols].astype(jnp.float32) + y).astype(jnp.bfloat16)

            @pl.when(k < chips)
            def _():
                o_copy(i, n, chip).start()

            @pl.when(k == chips)
            def _():
                o_local(n).start()

    def other(k):
        return (k - 1) + jnp.where(k - 1 >= chip, 1, 0)

    own_copy.wait()

    @pl.loop(0, chips + 1)
    def _(k):
        @pl.when(k == 0)
        def _():
            hidden(k, chip)
            mask_weights()

        @pl.when((k >= 1) & (k < chips))
        def _():
            j = other(k)
            x_copy((chip - j + chips) % chips).wait_recv()
            hidden(k, j)

            @pl.when(k == 1)
            def _():
                vn_copy(0, chip).wait_recv()

            vn_copy(k, j).wait_recv()

        @pl.when(k >= 1)
        def _():
            mix(k, jnp.where(k < chips, other(k), chip))

    for d in range(1, chips):
        x_copy(d).wait_send()
        src = (chip - d + chips) % chips
        for n in range(n_out):
            o_copy(src, n, chip).wait_send()
            o_copy(src, n, src).wait_recv()
    for n in range(n_out):
        o_local(n).wait()
    vn_copy(0, chip).wait_send()
    for k in range(1, chips):
        vn_copy(k, other(k)).wait_send()


def solution(mesh):
    row_spec = P('data', 'seq', None)
    chips = mesh.shape['seq'] // CORES

    def local_block(act_in, ln1_scale, ln1_bias, w_in, b_in, ln2_scale, ln2_bias, w_spatial, b_spatial, causal_mask, w_out, b_out):
        batch, rows, model = act_in.shape
        ffn = w_in.shape[1]
        gate = w_out.shape[0]
        seq = w_spatial.shape[0]
        span = CORES * rows
        assert batch == chips and span * chips == seq
        n_in, n_out = gate // NT, model // OT
        tiles = chips * (chips + 1) // 2
        hbm = pl.BlockSpec(memory_space=pl.ANY)
        vmem = pl.BlockSpec(memory_space=pltpu.VMEM)
        bf, f32 = jnp.bfloat16, jnp.float32
        dma = pltpu.SemaphoreType.DMA
        return pl.pallas_call(
            functools.partial(block_kernel, chips),
            out_shape=jax.ShapeDtypeStruct(act_in.shape, bf),
            in_specs=[hbm, vmem, vmem, hbm, vmem, vmem, vmem, hbm, vmem, hbm, hbm, vmem],
            out_specs=hbm,
            scratch_shapes=[
                pltpu.VMEM((model, ffn), bf),
                pltpu.VMEM((gate, model), bf),
                pltpu.VMEM((chips, rows, model), bf),
                pltpu.VMEM((rows, model), bf),
                pltpu.VMEM((rows, gate), bf),
                pltpu.VMEM((chips, rows, gate), bf),
                pltpu.VMEM((seq, gate), bf),
                pltpu.VMEM((chips, rows, seq), bf),
                pltpu.VMEM((tiles, rows, span), jnp.int32),
                pltpu.VMEM((rows, gate), bf),
                pltpu.VMEM((chips, rows, model), bf),
                pltpu.VMEM((chips, rows, 128), f32),
                dma((2 * n_in,)), dma, dma((chips,)), dma((tiles,)), dma,
                dma((chips,)), dma((chips,)), dma((chips,)), dma((chips,)),
                dma((chips, n_out)), dma((chips, n_out)), dma((n_out,)),
            ],
            compiler_params=pltpu.CompilerParams(collective_id=0, has_side_effects=True,
                                                 vmem_limit_bytes=66 * 1000 * 1000),
            name="gmlp_block",
        )(act_in, ln1_scale.reshape(1, -1), ln1_bias.reshape(1, -1), w_in, b_in.reshape(1, -1),
          ln2_scale.reshape(1, -1), ln2_bias.reshape(1, -1), w_spatial, b_spatial.reshape(-1, rows), causal_mask,
          w_out, b_out.reshape(1, -1))

    return jax.shard_map(local_block, mesh=mesh, in_specs=(row_spec,) + (P(),) * 11, out_specs=row_spec, check_vma=False)
```

time: 277 us -> 126 us (0.45)
  blocking collectives: 143 us -> 0 us
  Pallas kernels: 0 us -> 114 us
  local copies, waits for them, and re-layouts: 64.7 us -> 11.2 us
  matrix products: 52.7 us -> 0 us
  other arithmetic: 14.9 us -> 0 us
    all_to_all x2 -> x0, blocking collectives: 143 us -> none  [the longest x1 77.3 us: local_block(): spatial_rows = lax.all_to_all(spatial_cols, 'seq', 1, 2, tiled=True)]
    pallas_call x0 -> x1, Pallas kernels: none -> 114 us  [local_block(): pl.pallas_call(functools.partial(block_kernel, chips), out_shape=jax.Shap...]
    dot_general x3 -> x0, matrix products: 52.7 us -> none  [the longest x1 21.3 us: local_block(): jnp.einsum('bsd,df->bsf', normed, w_in, preferred_element_type=jnp.float32)]
    convert_element_type x4 -> x0, local copies, waits for them, and re-layouts: 42 us -> none  [the longest x2 22.6 us: local_block(): spatial_rows.astype(jnp.float32)]
    all_to_all x3 -> x0, local copies, waits for them, and re-layouts: 11.8 us -> none  [the longest x1 10.4 us: local_block(): spatial_rows = lax.all_to_all(spatial_cols, 'seq', 1, 2, tiled=True)]
    convert_element_type x2 -> x0, other arithmetic: 7.89 us -> none  [the longest x1 4.01 us: local_block(): layer_norm(hidden[:, :, gate_dim:].astype(jnp.float32), ln2_scale, ln2_bias)]
    reshape x0 -> x6, local copies, waits for them, and re-layouts: none -> 7.78 us  [the longest x1 1.31 us: local_block(): ln2_scale.reshape(1, -1)]
    unnamed x13 -> x1, local copies, waits for them, and re-layouts: 10.8 us -> 3.4 us
where the time goes in v1:
time: 126 us; the launch traced here: 125 us
  Pallas kernels  114 us (90%)
  local copies, waits for them, and re-layouts  11.2 us (9%)
    pallas_call x1, Pallas kernels, local_block(): pl.pallas_call(functools.partial(block_kernel, chips), out_shape=jax.Shap...  114 us
    unnamed x1, local copies, waits for them, and re-layouts  3.4 us

profile of v1, /device:TPU:81, one launch (start us, length us, event | category | flops | bytes accessed | tf_op | source)
XLA Modules:
  0.0 125.0 jit_solution(3137111872967677826)
XLA Ops:
  0.0 1.3 %reshape.21.ln1s = f32[1,1280]{1,0:T(1,128)} reshape(f32[1280]{0:T(1024)} %param.13) | data formatting | bytes 10240 | tf_op jit(solution)/shard_map/reshape | solution.py:280
  1.3 1.3 %reshape.22.ln1b = f32[1,1280]{1,0:T(1,128)} reshape(f32[1280]{0:T(1024)} %param.14) | data formatting | bytes 10240 | tf_op jit(solution)/shard_map/reshape | solution.py:280
  2.6 1.3 %reshape.27.b_out = f32[1,1280]{1,0:T(1,128)} reshape(f32[1280]{0:T(1024)} %param.23) | data formatting | bytes 10240 | tf_op jit(solution)/shard_map/reshape | solution.py:282
  3.9 1.3 %reshape.26.b_sp = f32[8,256]{1,0:T(8,128)} reshape(f32[2048]{0:T(1024)} %param.20) | data formatting | bytes 16384 | tf_op jit(solution)/shard_map/reshape | solution.py:281
  5.2 1.3 %reshape.24.ln2s = f32[1,2560]{1,0:T(1,128)} reshape(f32[2560]{0:T(1024)} %param.17) | data formatting | bytes 20480 | tf_op jit(solution)/shard_map/reshape | solution.py:281
  6.5 1.3 %reshape.25.ln2b = f32[1,2560]{1,0:T(1,128)} reshape(f32[2560]{0:T(1024)} %param.18) | data formatting | bytes 20480 | tf_op jit(solution)/shard_map/reshape | solution.py:281
  7.8 113.8 %gmlp_block.1 = bf16[4,256,1280]{2,1,0:T(8,128)(2,1)} custom-call(bf16[4,256,1280]{2,1,0:T(8,128)(2,1)} %x_hbm.1, f32[1,1280]{1,0:T(1,128)} %reshape.21.ln1s, f32[1,1280]{1,0:T(1,128)} %reshape.22.ln1b, bf16[1280,5120]{1,0:T(8,128)(2,1)} %w_in_hbm.1, f32[1,5120]{1,0:T(1,128)} %bitcast.1, f32[1,2560]{1,0:T(1,128)} %reshape.24.ln2s, f32[1,2560]{1,0:T(1,128)} %reshape.25.ln2b, ...), custom_call_target="tpu_custom_call" | custom-call | tf_op jit(solution)/shard_map/gmlp_block/pallas_call | solution.py:255
  121.6 3.4 %copy.14 = bf16[4,256,1280]{2,1,0:T(8,128)(2,1)} copy(bf16[4,256,1280]{2,1,0:T(8,128)(2,1)} %gmlp_block.1) | data formatting | bytes 5242880

commit v2 on v1

v2 whole, which is shorter than its diff:
```python
import functools

import jax
import jax.numpy as jnp
from jax import lax
from jax.experimental import pallas as pl
from jax.experimental.pallas import tpu as pltpu
from jax.sharding import PartitionSpec as P

LN_EPS = 1e-6
MESH = pl.DeviceIdType.MESH
GELU_A = 0.7978845608028654
GELU_B = 0.7978845608028654 * 0.044715
CORES = 2
NT = 512
OT = 256
PLANS = [
    [0, 1, 5, 3, 2, 6, 7, 4],
    [1, 0, 4, 2, 6, 3, 7, 5],
    [2, 1, 3, 0, 4, 5, 7, 6],
    [3, 0, 4, 2, 1, 5, 6, 7],
]


def gelu(a):
    return (0.5 * a) * (1.0 + jnp.tanh(a * (GELU_A + GELU_B * (a * a))))


def norm_rows(src, dst, at, groups, width, scale, shift):
    tiles = [slice(t * 128, (t + 1) * 128) for t in range(width // 128)]
    rows = [pl.ds(pl.multiple_of(at[0] + 32 * r, 32), 32) for r in range(groups)]
    to = [pl.ds(pl.multiple_of(at[1] + 32 * r, 32), 32) for r in range(groups)]

    def total(parts):
        acc = parts[0]
        for p in parts[1:]:
            acc = acc + p
        return jnp.sum(acc, axis=-1, keepdims=True) * (1.0 / width)

    def load(r, t):
        return src[r, t].astype(jnp.float32)

    mean = [total([load(r, t) for t in tiles]) for r in rows]
    inv = []
    for r, m in zip(rows, mean):
        inv.append(lax.rsqrt(total([(load(r, t) - m) * (load(r, t) - m) for t in tiles]) + LN_EPS))
    for r, m, s, d in zip(rows, mean, inv, to):
        for t in tiles:
            dst[d, t] = ((load(r, t) - m) * s * scale[:, t] + shift[:, t]).astype(jnp.bfloat16)


def by_chip(chip, values):
    out = values[-1]
    for c in range(len(values) - 1):
        out = jnp.where(chip == c, values[c], out)
    return out


def block_kernel(chips, x_hbm, ln1s_1d, ln1b_1d, w_in_hbm, b_in_1d, ln2s_1d, ln2b_1d, w_sp_hbm, b_sp_1d, mask_hbm,
                 w_out_hbm, b_out_1d, out_hbm,
                 w_in, w_out, xg, u, v, g, vn, wm, mk, q, o, bs, ln1s, ln1b, b_in, ln2s, ln2b, b_out,
                 w_in_sem, w_out_sem, wm_sem, mk_sem, own_sem, x_send, x_recv, v_send, v_recv, o_send, o_recv, o_loc):
    rows, model = x_hbm.shape[1:]
    gate = w_out.shape[0]
    n_in = gate // NT
    span = CORES * rows
    data = lax.axis_index("data")
    me = lax.axis_index("seq")
    chip = me // CORES
    core = me % CORES

    def device(c):
        return (data, c * CORES + core)

    partner = (data, chip * CORES + (1 - core))

    barrier = pltpu.get_barrier_semaphore()
    for d in range(1, chips):
        pl.semaphore_signal(barrier, inc=1, device_id=device((chip + d) % chips), device_id_type=MESH)
    pl.semaphore_signal(barrier, inc=1, device_id=partner, device_id_type=MESH)

    own_copy = pltpu.make_async_copy(x_hbm.at[chip], xg.at[chip], own_sem)
    own_copy.start()
    w_in_copies = []
    for n in range(2):
        cols = pl.ds(gate * (1 - n), gate)
        w_in_copies.append(pltpu.make_async_copy(w_in_hbm.at[:, cols], w_in.at[:, cols], w_in_sem.at[n]))
    w_in_copies[0].start()
    for src, dst in ((ln1s_1d, ln1s), (ln1b_1d, ln1b), (b_in_1d, b_in), (ln2s_1d, ln2s), (ln2b_1d, ln2b),
                     (b_out_1d, b_out)):
        dst[...] = src[...].reshape(1, -1)

    pl.semaphore_wait(barrier, chips)

    def x_copy(d):
        to = (chip + d) % chips
        return pltpu.make_async_remote_copy(
            src_ref=x_hbm.at[to], dst_ref=xg.at[chip], send_sem=x_send.at[d], recv_sem=x_recv.at[d],
            device_id=device(to), device_id_type=MESH)

    for d in (1, 3, 2):
        x_copy(d).start()

    w_in_copies[1].start()
    wm_copies, mk_copies = [], []
    t = 0
    for i in range(chips):
        r = pl.ds(pl.multiple_of((CORES * i + core) * rows, rows), rows)
        cp = pltpu.make_async_copy(w_sp_hbm.at[r, pl.ds(0, span * (i + 1))], wm.at[i, :, pl.ds(0, span * (i + 1))],
                                   wm_sem.at[i])
        cp.start()
        wm_copies.append(cp)
        for j in range(i + 1):
            cp = pltpu.make_async_copy(mask_hbm.at[r, pl.ds(span * j, span)], mk.at[t], mk_sem.at[t])
            cp.start()
            mk_copies.append(cp)
            t += 1
    w_out_copy = pltpu.make_async_copy(w_out_hbm, w_out, w_out_sem)
    w_out_copy.start()

    def vn_copy(j):
        r = pl.ds(pl.multiple_of((CORES * j + core) * rows, rows), rows)
        return pltpu.make_async_remote_copy(
            src_ref=vn.at[r], dst_ref=vn.at[r], send_sem=v_send.at[j], recv_sem=v_recv.at[j],
            device_id=partner, device_id_type=MESH)

    def hidden(k, j):
        @pl.when(k == 0)
        def _():
            own_copy.wait()
            w_in_copies[0].wait()

        @pl.when(k > 0)
        def _():
            x_copy((chip - j + chips) % chips).wait_recv()

        norm_rows(xg.at[j], u, (0, 0), rows // 32, model, ln1s, ln1b)

        def half(dst, base, n):
            cols = slice(n * NT, (n + 1) * NT)
            wcols = slice(base + n * NT, base + (n + 1) * NT)
            a = jnp.dot(u[...], w_in[:, wcols], preferred_element_type=jnp.float32) + b_in[:, wcols]
            dst[:, cols] = gelu(a).astype(jnp.bfloat16)

        for n in range(n_in):
            half(v, gate, n)

        own_rows = (CORES * j + core) * rows

        @pl.loop(0, 2)
        def _(r):
            norm_rows(v, vn, (r * 128, own_rows + r * 128), 4, gate, ln2s, ln2b)

        @pl.when(k == 0)
        def _():
            w_in_copies[1].wait()

        half(g.at[j], 0, 0)
        vn_copy(j).start()
        for n in range(1, n_in):
            half(g.at[j], 0, n)

    def mask_weights():
        for cp in wm_copies + mk_copies:
            cp.wait()
        t = 0
        for i in range(chips):
            for j in range(i + 1):
                cols = pl.ds(span * j, span)

                @pl.loop(0, rows // 32)
                def _(r, i=i, t=t, cols=cols):
                    rr = pl.ds(pl.multiple_of(r * 32, 32), 32)
                    w = wm[i, rr, cols].astype(jnp.float32)
                    wm[i, rr, cols] = jnp.where(mk[t, rr, :] > 0, w, 0.0).astype(jnp.bfloat16)

                t += 1
            row = b_sp_1d[pl.ds(pl.multiple_of((CORES * i + core) * rows, rows), rows)].reshape(1, rows)
            bs[i, :, :] = jnp.transpose(jnp.broadcast_to(row, (128, rows)))

    cuts = [(0, 768), (768, model)] if model > 768 else [(0, model)]

    def o_copy(i, n, recv):
        cols = pl.ds(cuts[n][0], cuts[n][1] - cuts[n][0])
        return pltpu.make_async_remote_copy(
            src_ref=o.at[i, :, cols], dst_ref=out_hbm.at[chip, :, cols], send_sem=o_send.at[i, n],
            recv_sem=o_recv.at[recv, n], device_id=device(i), device_id_type=MESH)

    def o_local(n):
        cols = pl.ds(cuts[n][0], cuts[n][1] - cuts[n][0])
        return pltpu.make_async_copy(o.at[chip, :, cols], out_hbm.at[chip, :, cols], o_loc.at[n])

    def mix(i):
        @pl.when(i != chip)
        def _():
            vn_copy(i).wait_recv()

        @pl.when(i == chip + 1)
        def _():
            vn_copy(chip).wait_recv()

        @pl.when((i == chip) & (i == chips - 1))
        def _():
            vn_copy(chip).wait_recv()

        for s in range(chips):
            @pl.when(i == s)
            def _(s=s):
                depth = span * (s + 1)
                for n in range(n_in):
                    cols = slice(n * NT, (n + 1) * NT)
                    acc = jnp.dot(wm[s, :, :depth], vn[:depth, cols], preferred_element_type=jnp.float32)
                    sp = (acc + bs[s, :, 0:1]).astype(jnp.bfloat16).astype(jnp.float32)
                    q[:, cols] = (g[s, :, cols].astype(jnp.float32) * sp).astype(jnp.bfloat16)

        for n, (lo, hi) in enumerate(cuts):
            for c in range(lo, hi, OT):
                cols = slice(c, c + OT)
                y = jnp.dot(q[...], w_out[:, cols], preferred_element_type=jnp.float32) + b_out[:, cols]
                o[i, :, cols] = (xg[i, :, cols].astype(jnp.float32) + y).astype(jnp.bfloat16)

            @pl.when(i != chip)
            def _(n=n):
                o_copy(i, n, chip).start()

            @pl.when(i == chip)
            def _(n=n):
                o_local(n).start()

    plans = by_chip(chip, [sum(op << (3 * k) for k, op in enumerate(p)) for p in PLANS])

    @pl.loop(0, 2 * chips)
    def _(k):
        op = lax.shift_right_logical(plans, 3 * k) % 8

        @pl.when(op < chips)
        def _():
            hidden(k, op)

        @pl.when(k == 0)
        def _():
            mask_weights()
            w_out_copy.wait()

        @pl.when(op >= chips)
        def _():
            mix(op - chips)

    for d in range(1, chips):
        x_copy(d).wait_send()
        src = (chip - d + chips) % chips
        for n in range(len(cuts)):
            o_copy(src, n, chip).wait_send()
            o_copy(src, n, src).wait_recv()
    for n in range(len(cuts)):
        o_local(n).wait()
    for j in range(chips):
        vn_copy(j).wait_send()


def solution(mesh):
    row_spec = P('data', 'seq', None)
    chips = mesh.shape['seq'] // CORES

    def local_block(act_in, ln1_scale, ln1_bias, w_in, b_in, ln2_scale, ln2_bias, w_spatial, b_spatial, causal_mask, w_out, b_out):
        batch, rows, model = act_in.shape
        ffn = w_in.shape[1]
        gate = w_out.shape[0]
        seq = w_spatial.shape[0]
        span = CORES * rows
        assert batch == chips and span * chips == seq
        n_out = 2 if model > 768 else 1
        tiles = chips * (chips + 1) // 2
        hbm = pl.BlockSpec(memory_space=pl.ANY)
        vmem = pl.BlockSpec(memory_space=pltpu.VMEM)
        bf, f32 = jnp.bfloat16, jnp.float32
        dma = pltpu.SemaphoreType.DMA
        return pl.pallas_call(
            functools.partial(block_kernel, chips),
            out_shape=jax.ShapeDtypeStruct(act_in.shape, bf),
            in_specs=[hbm, vmem, vmem, hbm, vmem, vmem, vmem, hbm, vmem, hbm, hbm, vmem],
            out_specs=hbm,
            scratch_shapes=[
                pltpu.VMEM((model, ffn), bf),
                pltpu.VMEM((gate, model), bf),
                pltpu.VMEM((chips, rows, model), bf),
                pltpu.VMEM((rows, model), bf),
                pltpu.VMEM((rows, gate), bf),
                pltpu.VMEM((chips, rows, gate), bf),
                pltpu.VMEM((seq, gate), bf),
                pltpu.VMEM((chips, rows, seq), bf),
                pltpu.VMEM((tiles, rows, span), jnp.int32),
                pltpu.VMEM((rows, gate), bf),
                pltpu.VMEM((chips, rows, model), bf),
                pltpu.VMEM((chips, rows, 128), f32),
                pltpu.VMEM((1, model), f32),
                pltpu.VMEM((1, model), f32),
                pltpu.VMEM((1, ffn), f32),
                pltpu.VMEM((1, gate), f32),
                pltpu.VMEM((1, gate), f32),
                pltpu.VMEM((1, model), f32),
                dma((2,)), dma, dma((chips,)), dma((tiles,)), dma,
                dma((chips,)), dma((chips,)), dma((chips,)), dma((chips,)),
                dma((chips, n_out)), dma((chips, n_out)), dma((n_out,)),
            ],
            compiler_params=pltpu.CompilerParams(collective_id=0, has_side_effects=True,
                                                 vmem_limit_bytes=66 * 1000 * 1000),
            name="gmlp_block",
        )(act_in, ln1_scale, ln1_bias, w_in, b_in, ln2_scale, ln2_bias, w_spatial, b_spatial, causal_mask, w_out, b_out)

    return jax.shard_map(local_block, mesh=mesh, in_specs=(row_spec,) + (P(),) * 11, out_specs=row_spec, check_vma=False)
```

time: 126 us -> 86 us (0.68)
  Pallas kernels: 114 us -> 81.7 us
  local copies, waits for them, and re-layouts: 11.2 us -> 3.4 us
    pallas_call x1, Pallas kernels: 114 us -> 81.7 us  [local_block(): pl.pallas_call(functools.partial(block_kernel, chips), out_shape=jax.Shap...]
    reshape x6 -> x0, local copies, waits for them, and re-layouts: 7.78 us -> none  [the longest x1 1.31 us: local_block(): ln2_scale.reshape(1, -1)]
where the time goes in v2:
time: 86 us; the launch traced here: 85.1 us
  Pallas kernels  81.7 us (95%)
  local copies, waits for them, and re-layouts  3.4 us (4%)
    pallas_call x1, Pallas kernels, local_block(): pl.pallas_call(functools.partial(block_kernel, chips), out_shape=jax.Shap...  81.7 us
    unnamed x1, local copies, waits for them, and re-layouts  3.4 us

profile of v2, /device:TPU:81, one launch (start us, length us, event | category | flops | bytes accessed | tf_op | source)
XLA Modules:
  0.0 85.1 jit_solution(18356986783884967386)
XLA Ops:
  0.0 81.7 %gmlp_block.1 = bf16[4,256,1280]{2,1,0:T(8,128)(2,1)} custom-call(bf16[4,256,1280]{2,1,0:T(8,128)(2,1)} %x_hbm.1, f32[1280]{0:T(1024)} %ln1s_1d.1, f32[1280]{0:T(1024)} %ln1b_1d.1, bf16[1280,5120]{1,0:T(8,128)(2,1)} %w_in_hbm.1, f32[5120]{0:T(1024)} %b_in_1d.1, f32[2560]{0:T(1024)} %ln2s_1d.1, f32[2560]{0:T(1024)} %ln2b_1d.1, bf16[2048,2048]{1,0:T(8,128)(2,1)} %w_sp_hbm.1, ...), custom_call_target="tpu_custom_call" | custom-call | tf_op jit(solution)/shard_map/gmlp_block/pallas_call | solution.py:278
  81.7 3.4 %copy.14 = bf16[4,256,1280]{2,1,0:T(8,128)(2,1)} copy(bf16[4,256,1280]{2,1,0:T(8,128)(2,1)} %gmlp_block.1) | data formatting | bytes 5242880

commit v3 on v2

--- a/solution.py
+++ b/solution.py
@@ -15,10 +15,24 @@
 NT = 512
 OT = 256
 PLANS = [
-    [0, 1, 5, 3, 2, 6, 7, 4],
-    [1, 0, 4, 2, 6, 3, 7, 5],
-    [2, 1, 3, 0, 4, 5, 7, 6],
-    [3, 0, 4, 2, 1, 5, 6, 7],
+    [0, 4, 3, 1, 2, 5, 7, 6],
+    [0, 4, 3, 1, 2, 7, 5, 6],
+    [1, 0, 2, 4, 6, 5, 3, 7],
+    [1, 0, 2, 4, 6, 5, 3, 7],
+    [2, 1, 3, 0, 7, 5, 6, 4],
+    [2, 1, 3, 0, 7, 5, 6, 4],
+    [3, 0, 2, 1, 5, 4, 6, 7],
+    [3, 2, 0, 1, 4, 6, 5, 7],
+]
+SENDS = [
+    [(1, 0), (3, 0), (2, 0)],
+    [(1, 0), (3, 0), (2, 0)],
+    [(1, 0), (3, 0), (2, 0)],
+    [(1, 0), (3, 0), (2, 0)],
+    [(1, 0), (3, 0), (2, 0)],
+    [(1, 0), (3, 0), (2, 0)],
+    [(1, 0), (3, 0), (2, 0)],
+    [(1, 0), (3, 0), (2, 0)],
 ]
 
 
@@ -49,11 +63,25 @@
             dst[d, t] = ((load(r, t) - m) * s * scale[:, t] + shift[:, t]).astype(jnp.bfloat16)
 
 
-def by_chip(chip, values):
+def pick(me, values):
     out = values[-1]
-    for c in range(len(values) - 1):
-        out = jnp.where(chip == c, values[c], out)
+    for d in range(len(values) - 1):
+        out = jnp.where(me == d, values[d], out)
     return out
+
+
+def packed(fields, bits):
+    return sum(f << (bits * k) for k, f in enumerate(fields))
+
+
+def partner_waits(plan, chips):
+    seen, waits = set(), []
+    for op in plan:
+        need = set(range(op - chips + 1)) - seen if op >= chips else set()
+        seen |= need
+        waits.append(sum(1 << j for j in need))
+    assert seen == set(range(chips)) and waits[0] == 0
+    return waits[1:]
 
 
 def block_kernel(chips, x_hbm, ln1s_1d, ln1b_1d, w_in_hbm, b_in_1d, ln2s_1d, ln2b_1d, w_sp_hbm, b_sp_1d, mask_hbm,
@@ -98,8 +126,17 @@
             src_ref=x_hbm.at[to], dst_ref=xg.at[chip], send_sem=x_send.at[d], recv_sem=x_recv.at[d],
             device_id=device(to), device_id_type=MESH)
 
-    for d in (1, 3, 2):
-        x_copy(d).start()
+    sends = pick(me, [packed([d + (late << 2) for d, late in p], 3) for p in SENDS])
+
+    def start_sends(late):
+        for slot in range(chips - 1):
+            field = lax.shift_right_logical(sends, 3 * slot) % 8
+
+            @pl.when(field // 4 == late)
+            def _(field=field):
+                x_copy(field % 4).start()
+
+    start_sends(0)
 
     w_in_copies[1].start()
     wm_copies, mk_copies = [], []
@@ -190,18 +227,11 @@
         cols = pl.ds(cuts[n][0], cuts[n][1] - cuts[n][0])
         return pltpu.make_async_copy(o.at[chip, :, cols], out_hbm.at[chip, :, cols], o_loc.at[n])
 
-    def mix(i):
-        @pl.when(i != chip)
-        def _():
-            vn_copy(i).wait_recv()
-
-        @pl.when(i == chip + 1)
-        def _():
-            vn_copy(chip).wait_recv()
-
-        @pl.when((i == chip) & (i == chips - 1))
-        def _():
-            vn_copy(chip).wait_recv()
+    def mix(i, waits):
+        for j in range(chips):
+            @pl.when(lax.shift_right_logical(waits, j) % 2 == 1)
+            def _(j=j):
+                vn_copy(j).wait_recv()
 
         for s in range(chips):
             @pl.when(i == s)
@@ -227,11 +257,12 @@
             def _(n=n):
                 o_local(n).start()
 
-    plans = by_chip(chip, [sum(op << (3 * k) for k, op in enumerate(p)) for p in PLANS])
+    plan = pick(me, [packed(p, 3) for p in PLANS])
+    plan_waits = pick(me, [packed(partner_waits(p, chips), chips) for p in PLANS])
 
     @pl.loop(0, 2 * chips)
     def _(k):
-        op = lax.shift_right_logical(plans, 3 * k) % 8
+        op = lax.shift_right_logical(plan, 3 * k) % 8
 
         @pl.when(op < chips)
         def _():
@@ -239,12 +270,13 @@
 
         @pl.when(k == 0)
         def _():
+            start_sends(1)
             mask_weights()
             w_out_copy.wait()
 
         @pl.when(op >= chips)
         def _():
-            mix(op - chips)
+            mix(op - chips, lax.shift_right_logical(plan_waits, chips * (k - 1)) % (1 << chips))
 
     for d in range(1, chips):
         x_copy(d).wait_send()
@@ -270,6 +302,7 @@
         span = CORES * rows
         assert batch == chips and span * chips == seq
         n_out = 2 if model > 768 else 1
+        assert chips == 4 and len(PLANS) == len(SENDS) == CORES * chips
         tiles = chips * (chips + 1) // 2
         hbm = pl.BlockSpec(memory_space=pl.ANY)
         vmem = pl.BlockSpec(memory_space=pltpu.VMEM)
@@ -277,7 +310,7 @@
         dma = pltpu.SemaphoreType.DMA
         return pl.pallas_call(
             functools.partial(block_kernel, chips),
-            out_shape=jax.ShapeDtypeStruct(act_in.shape, bf),
+            out_shape=pltpu.VMEM(act_in.shape, bf),
             in_specs=[hbm, vmem, vmem, hbm, vmem, vmem, vmem, hbm, vmem, hbm, hbm, vmem],
             out_specs=hbm,
             scratch_shapes=[
@@ -304,7 +337,7 @@
                 dma((chips, n_out)), dma((chips, n_out)), dma((n_out,)),
             ],
             compiler_params=pltpu.CompilerParams(collective_id=0, has_side_effects=True,
-                                                 vmem_limit_bytes=66 * 1000 * 1000),
+                                                 vmem_limit_bytes=62 * 1000 * 1000),
             name="gmlp_block",
         )(act_in, ln1_scale, ln1_bias, w_in, b_in, ln2_scale, ln2_bias, w_spatial, b_spatial, causal_mask, w_out, b_out)
 

time: 86 us -> 79.8 us (0.928)
  Pallas kernels: 81.7 us -> 78.1 us
  local copies, waits for them, and re-layouts: 3.4 us -> 1.49 us
    pallas_call x1, Pallas kernels: 81.7 us -> 78.1 us  [local_block(): pl.pallas_call(functools.partial(block_kernel, chips), out_shape=pltpu.VM...]
    unnamed x1, local copies, waits for them, and re-layouts: 3.4 us -> 1.49 us
where the time goes in v3:
time: 79.8 us; the launch traced here: 79.6 us
  Pallas kernels  78.1 us (98%)
  local copies, waits for them, and re-layouts  1.49 us (2%)
    pallas_call x1, Pallas kernels, local_block(): pl.pallas_call(functools.partial(block_kernel, chips), out_shape=pltpu.VM...  78.1 us

profile of v3, /device:TPU:81, one launch (start us, length us, event | category | flops | bytes accessed | tf_op | source)
XLA Modules:
  0.0 79.6 jit_solution(4253369502715506517)
XLA Ops:
  0.0 78.1 %gmlp_block.1 = bf16[4,256,1280]{2,1,0:T(8,128)(2,1)S(1)} custom-call(bf16[4,256,1280]{2,1,0:T(8,128)(2,1)} %x_hbm.1, f32[1280]{0:T(1024)} %ln1s_1d.1, f32[1280]{0:T(1024)} %ln1b_1d.1, bf16[1280,5120]{1,0:T(8,128)(2,1)} %w_in_hbm.1, f32[5120]{0:T(1024)} %b_in_1d.1, f32[2560]{0:T(1024)} %ln2s_1d.1, f32[2560]{0:T(1024)} %ln2b_1d.1, ...), custom_call_target="tpu_custom_call" | custom-call | tf_op jit(solution)/shard_map/gmlp_block/pallas_call | solution.py:311
  78.1 1.5 %copy.14 = bf16[4,256,1280]{2,1,0:T(8,128)(2,1)} copy(bf16[4,256,1280]{2,1,0:T(8,128)(2,1)S(1)} %gmlp_block.1) | data formatting | bytes 5242880

commit v4 on v3

--- a/solution.py
+++ b/solution.py
@@ -12,27 +12,28 @@
 GELU_A = 0.7978845608028654
 GELU_B = 0.7978845608028654 * 0.044715
 CORES = 2
+HT = 256
 NT = 512
 OT = 256
 PLANS = [
-    [0, 4, 3, 1, 2, 5, 7, 6],
-    [0, 4, 3, 1, 2, 7, 5, 6],
-    [1, 0, 2, 4, 6, 5, 3, 7],
-    [1, 0, 2, 4, 6, 5, 3, 7],
-    [2, 1, 3, 0, 7, 5, 6, 4],
-    [2, 1, 3, 0, 7, 5, 6, 4],
-    [3, 0, 2, 1, 5, 4, 6, 7],
-    [3, 2, 0, 1, 4, 6, 5, 7],
+    [0, 1, 3, 2, 6, 5, 7, 4],
+    [0, 1, 3, 2, 6, 5, 7, 4],
+    [1, 0, 2, 3, 7, 6, 4, 5],
+    [1, 0, 2, 3, 7, 6, 4, 5],
+    [2, 1, 0, 4, 3, 5, 7, 6],
+    [2, 1, 0, 4, 3, 5, 7, 6],
+    [3, 0, 1, 5, 2, 6, 4, 7],
+    [3, 0, 1, 5, 2, 6, 4, 7],
 ]
 SENDS = [
-    [(1, 0), (3, 0), (2, 0)],
-    [(1, 0), (3, 0), (2, 0)],
-    [(1, 0), (3, 0), (2, 0)],
-    [(1, 0), (3, 0), (2, 0)],
-    [(1, 0), (3, 0), (2, 0)],
-    [(1, 0), (3, 0), (2, 0)],
-    [(1, 0), (3, 0), (2, 0)],
-    [(1, 0), (3, 0), (2, 0)],
+    [(1, 0), (3, 0), (2, 2)],
+    [(3, 0), (1, 1), (2, 2)],
+    [(3, 0), (1, 0), (2, 1)],
+    [(1, 0), (3, 1), (2, 2)],
+    [(3, 0), (1, 0), (2, 1)],
+    [(1, 0), (3, 1), (2, 2)],
+    [(3, 0), (1, 0), (2, 0)],
+    [(3, 0), (1, 1), (2, 2)],
 ]
 
 
@@ -74,20 +75,22 @@
     return sum(f << (bits * k) for k, f in enumerate(fields))
 
 
-def partner_waits(plan, chips):
+def partner_waits(plan, chips, core):
     seen, waits = set(), []
-    for op in plan:
-        need = set(range(op - chips + 1)) - seen if op >= chips else set()
+    for k, op in enumerate(plan):
+        need = set(range(op - chips + core)) - seen if op >= chips else set()
+        if k == len(plan) - 1:
+            need = set(range(chips)) - seen
         seen |= need
         waits.append(sum(1 << j for j in need))
-    assert seen == set(range(chips)) and waits[0] == 0
+    assert waits[0] == 0
     return waits[1:]
 
 
 def block_kernel(chips, x_hbm, ln1s_1d, ln1b_1d, w_in_hbm, b_in_1d, ln2s_1d, ln2b_1d, w_sp_hbm, b_sp_1d, mask_hbm,
                  w_out_hbm, b_out_1d, out_hbm,
-                 w_in, w_out, xg, u, v, g, vn, wm, mk, q, o, bs, ln1s, ln1b, b_in, ln2s, ln2b, b_out,
-                 w_in_sem, w_out_sem, wm_sem, mk_sem, own_sem, x_send, x_recv, v_send, v_recv, o_send, o_recv, o_loc):
+                 w_in, w_out, xg, xs, u, v, g, vn, wm, mk, q, o, bs, ln1s, ln1b, b_in, ln2s, ln2b, b_out,
+                 w_in_sem, w_out_sem, wm_sem, mk_sem, own_sem, xs_sem, x_send, x_recv, v_send, v_recv, o_send, o_recv, o_loc):
     rows, model = x_hbm.shape[1:]
     gate = w_out.shape[0]
     n_in = gate // NT
@@ -120,25 +123,27 @@
 
     pl.semaphore_wait(barrier, chips)
 
-    def x_copy(d):
+    def x_copy(d, src):
         to = (chip + d) % chips
         return pltpu.make_async_remote_copy(
-            src_ref=x_hbm.at[to], dst_ref=xg.at[chip], send_sem=x_send.at[d], recv_sem=x_recv.at[d],
+            src_ref=src.at[to], dst_ref=xg.at[chip], send_sem=x_send.at[d], recv_sem=x_recv.at[d],
             device_id=device(to), device_id_type=MESH)
 
-    sends = pick(me, [packed([d + (late << 2) for d, late in p], 3) for p in SENDS])
-
-    def start_sends(late):
+    sends = pick(me, [packed([d + (stage << 2) for d, stage in p], 4) for p in SENDS])
+
+    def start_sends(stage):
         for slot in range(chips - 1):
-            field = lax.shift_right_logical(sends, 3 * slot) % 8
-
-            @pl.when(field // 4 == late)
+            field = lax.shift_right_logical(sends, 4 * slot) % 16
+
+            @pl.when(field // 4 == (0 if stage is None else stage))
             def _(field=field):
-                x_copy(field % 4).start()
-
-    start_sends(0)
-
+                x_copy(field % 4, x_hbm if stage is None else xs).start()
+
+    start_sends(None)
+    xs_copy = pltpu.make_async_copy(x_hbm, xs, xs_sem)
+    xs_copy.start()
     w_in_copies[1].start()
+
     wm_copies, mk_copies = [], []
     t = 0
     for i in range(chips):
@@ -161,7 +166,7 @@
             src_ref=vn.at[r], dst_ref=vn.at[r], send_sem=v_send.at[j], recv_sem=v_recv.at[j],
             device_id=partner, device_id_type=MESH)
 
-    def hidden(k, j):
+    def hidden(k, h, j):
         @pl.when(k == 0)
         def _():
             own_copy.wait()
@@ -169,33 +174,37 @@
 
         @pl.when(k > 0)
         def _():
-            x_copy((chip - j + chips) % chips).wait_recv()
+            x_copy((chip - j + chips) % chips, xs).wait_recv()
 
         norm_rows(xg.at[j], u, (0, 0), rows // 32, model, ln1s, ln1b)
 
-        def half(dst, base, n):
-            cols = slice(n * NT, (n + 1) * NT)
-            wcols = slice(base + n * NT, base + (n + 1) * NT)
-            a = jnp.dot(u[...], w_in[:, wcols], preferred_element_type=jnp.float32) + b_in[:, wcols]
-            dst[:, cols] = gelu(a).astype(jnp.bfloat16)
-
-        for n in range(n_in):
-            half(v, gate, n)
+        def half(dst, base, first, last):
+            def finish(n, a):
+                a = a + b_in[:, base + n * HT:base + (n + 1) * HT]
+                dst[:, n * HT:(n + 1) * HT] = gelu(a).astype(jnp.bfloat16)
+
+            held = None
+            for n in range(first, last):
+                a = jnp.dot(u[...], w_in[:, base + n * HT:base + (n + 1) * HT], preferred_element_type=jnp.float32)
+                if held is not None:
+                    finish(n - 1, held)
+                held = a
+            finish(last - 1, held)
+
+        half(v, gate, 0, gate // HT)
 
         own_rows = (CORES * j + core) * rows
 
-        @pl.loop(0, 2)
-        def _(r):
-            norm_rows(v, vn, (r * 128, own_rows + r * 128), 4, gate, ln2s, ln2b)
-
         @pl.when(k == 0)
         def _():
             w_in_copies[1].wait()
-
-        half(g.at[j], 0, 0)
+            xs_copy.wait()
+
+        norm_rows(v, vn, (0, own_rows), rows // 32, gate, ln2s, ln2b)
+        half(g.at[j], 0, 0, 5)
         vn_copy(j).start()
-        for n in range(1, n_in):
-            half(g.at[j], 0, n)
+        start_sends(h + 1)
+        half(g.at[j], 0, 5, gate // HT)
 
     def mask_weights():
         for cp in wm_copies + mk_copies:
@@ -233,10 +242,9 @@
             def _(j=j):
                 vn_copy(j).wait_recv()
 
-        for s in range(chips):
-            @pl.when(i == s)
-            def _(s=s):
-                depth = span * (s + 1)
+        for s, c in [(s, c) for s in range(chips) for c in range(CORES)]:
+            @pl.when((i == s) & (core == c))
+            def _(s=s, depth=span * s + rows * (c + 1)):
                 for n in range(n_in):
                     cols = slice(n * NT, (n + 1) * NT)
                     acc = jnp.dot(wm[s, :, :depth], vn[:depth, cols], preferred_element_type=jnp.float32)
@@ -258,7 +266,8 @@
                 o_local(n).start()
 
     plan = pick(me, [packed(p, 3) for p in PLANS])
-    plan_waits = pick(me, [packed(partner_waits(p, chips), chips) for p in PLANS])
+    counts = pick(me, [packed([sum(o < chips for o in p[:k]) % 4 for k in range(len(p))], 2) for p in PLANS])
+    plan_waits = pick(me, [packed(partner_waits(p, chips, d % CORES), chips) for d, p in enumerate(PLANS)])
 
     @pl.loop(0, 2 * chips)
     def _(k):
@@ -266,11 +275,10 @@
 
         @pl.when(op < chips)
         def _():
-            hidden(k, op)
+            hidden(k, lax.shift_right_logical(counts, 2 * k) % 4, op)
 
         @pl.when(k == 0)
         def _():
-            start_sends(1)
             mask_weights()
             w_out_copy.wait()
 
@@ -279,7 +287,7 @@
             mix(op - chips, lax.shift_right_logical(plan_waits, chips * (k - 1)) % (1 << chips))
 
     for d in range(1, chips):
-        x_copy(d).wait_send()
+        x_copy(d, xs).wait_send()
         src = (chip - d + chips) % chips
         for n in range(len(cuts)):
             o_copy(src, n, chip).wait_send()
@@ -317,6 +325,7 @@
                 pltpu.VMEM((model, ffn), bf),
                 pltpu.VMEM((gate, model), bf),
                 pltpu.VMEM((chips, rows, model), bf),
+                pltpu.VMEM((chips, rows, model), bf),
                 pltpu.VMEM((rows, model), bf),
                 pltpu.VMEM((rows, gate), bf),
                 pltpu.VMEM((chips, rows, gate), bf),
@@ -332,7 +341,7 @@
                 pltpu.VMEM((1, gate), f32),
                 pltpu.VMEM((1, gate), f32),
                 pltpu.VMEM((1, model), f32),
-                dma((2,)), dma, dma((chips,)), dma((tiles,)), dma,
+                dma((2,)), dma, dma((chips,)), dma((tiles,)), dma, dma,
                 dma((chips,)), dma((chips,)), dma((chips,)), dma((chips,)),
                 dma((chips, n_out)), dma((chips, n_out)), dma((n_out,)),
             ],

time: 79.8 us -> 77.5 us (0.971)
  Pallas kernels: 78.1 us -> 75.8 us
    pallas_call x1, Pallas kernels: 78.1 us -> 75.8 us  [local_block(): pl.pallas_call(functools.partial(block_kernel, chips), out_shape=pltpu.VM...]
where the time goes in v4:
time: 77.5 us; the launch traced here: 77.3 us
  Pallas kernels  75.8 us (98%)
  local copies, waits for them, and re-layouts  1.49 us (2%)
    pallas_call x1, Pallas kernels, local_block(): pl.pallas_call(functools.partial(block_kernel, chips), out_shape=pltpu.VM...  75.8 us

profile of v4, /device:TPU:81, one launch (start us, length us, event | category | flops | bytes accessed | tf_op | source)
XLA Modules:
  0.0 77.3 jit_solution(8844294849374953124)
XLA Ops:
  0.0 75.8 %gmlp_block.1 = bf16[4,256,1280]{2,1,0:T(8,128)(2,1)S(1)} custom-call(bf16[4,256,1280]{2,1,0:T(8,128)(2,1)} %x_hbm.1, f32[1280]{0:T(1024)} %ln1s_1d.1, f32[1280]{0:T(1024)} %ln1b_1d.1, bf16[1280,5120]{1,0:T(8,128)(2,1)} %w_in_hbm.1, f32[5120]{0:T(1024)} %b_in_1d.1, f32[2560]{0:T(1024)} %ln2s_1d.1, f32[2560]{0:T(1024)} %ln2b_1d.1, ...), custom_call_target="tpu_custom_call" | custom-call | tf_op jit(solution)/shard_map/gmlp_block/pallas_call | solution.py:319
  75.8 1.5 %copy.14 = bf16[4,256,1280]{2,1,0:T(8,128)(2,1)} copy(bf16[4,256,1280]{2,1,0:T(8,128)(2,1)S(1)} %gmlp_block.1) | data formatting | bytes 5242880

commit v5 on v4

--- a/solution.py
+++ b/solution.py
@@ -16,24 +16,24 @@
 NT = 512
 OT = 256
 PLANS = [
-    [0, 1, 3, 2, 6, 5, 7, 4],
-    [0, 1, 3, 2, 6, 5, 7, 4],
-    [1, 0, 2, 3, 7, 6, 4, 5],
-    [1, 0, 2, 3, 7, 6, 4, 5],
-    [2, 1, 0, 4, 3, 5, 7, 6],
-    [2, 1, 0, 4, 3, 5, 7, 6],
-    [3, 0, 1, 5, 2, 6, 4, 7],
-    [3, 0, 1, 5, 2, 6, 4, 7],
+    [0, 1, 4, 2, 6, 3, 7, 5],
+    [0, 1, 4, 2, 6, 3, 7, 5],
+    [1, 2, 0, 3, 7, 6, 4, 5],
+    [1, 2, 0, 3, 7, 6, 4, 5],
+    [2, 1, 0, 4, 3, 7, 5, 6],
+    [2, 1, 0, 4, 3, 7, 5, 6],
+    [3, 0, 1, 5, 2, 4, 6, 7],
+    [3, 0, 1, 5, 2, 4, 6, 7],
 ]
 SENDS = [
-    [(1, 0), (3, 0), (2, 2)],
     [(3, 0), (1, 1), (2, 2)],
-    [(3, 0), (1, 0), (2, 1)],
     [(1, 0), (3, 1), (2, 2)],
-    [(3, 0), (1, 0), (2, 1)],
+    [(3, 0), (1, 0), (2, 2)],
     [(1, 0), (3, 1), (2, 2)],
-    [(3, 0), (1, 0), (2, 0)],
-    [(3, 0), (1, 1), (2, 2)],
+    [(2, 0), (3, 0), (1, 1)],
+    [(2, 0), (3, 1), (1, 2)],
+    [(3, 0), (1, 2), (2, 2)],
+    [(3, 0), (2, 2), (1, 2)],
 ]
 
 
@@ -131,17 +131,15 @@
 
     sends = pick(me, [packed([d + (stage << 2) for d, stage in p], 4) for p in SENDS])
 
-    def start_sends(stage):
+    def start_sends(stage, src):
         for slot in range(chips - 1):
             field = lax.shift_right_logical(sends, 4 * slot) % 16
 
-            @pl.when(field // 4 == (0 if stage is None else stage))
+            @pl.when(field // 4 == stage)
             def _(field=field):
-                x_copy(field % 4, x_hbm if stage is None else xs).start()
-
-    start_sends(None)
-    xs_copy = pltpu.make_async_copy(x_hbm, xs, xs_sem)
-    xs_copy.start()
+                x_copy(field % 4, src).start()
+
+    start_sends(0, x_hbm)
     w_in_copies[1].start()
 
     wm_copies, mk_copies = [], []
@@ -159,6 +157,8 @@
             t += 1
     w_out_copy = pltpu.make_async_copy(w_out_hbm, w_out, w_out_sem)
     w_out_copy.start()
+    xs_copy = pltpu.make_async_copy(x_hbm, xs, xs_sem)
+    xs_copy.start()
 
     def vn_copy(j):
         r = pl.ds(pl.multiple_of((CORES * j + core) * rows, rows), rows)
@@ -198,12 +198,23 @@
         @pl.when(k == 0)
         def _():
             w_in_copies[1].wait()
-            xs_copy.wait()
 
         norm_rows(v, vn, (0, own_rows), rows // 32, gate, ln2s, ln2b)
         half(g.at[j], 0, 0, 5)
         vn_copy(j).start()
-        start_sends(h + 1)
+
+        @pl.when(h == 0)
+        def _():
+            start_sends(1, x_hbm)
+
+        @pl.when(h == 1)
+        def _():
+            xs_copy.wait()
+
+        @pl.when(h > 0)
+        def _():
+            start_sends(h + 1, xs)
+
         half(g.at[j], 0, 5, gate // HT)
 
     def mask_weights():

time: 77.5 us -> 75.5 us (0.974)
  Pallas kernels: 75.8 us -> 73.9 us
    pallas_call x1, Pallas kernels: 75.8 us -> 73.9 us  [local_block(): pl.pallas_call(functools.partial(block_kernel, chips), out_shape=pltpu.VM...]
where the time goes in v5:
time: 75.5 us; the launch traced here: 75.4 us
  Pallas kernels  73.9 us (98%)
  local copies, waits for them, and re-layouts  1.49 us (2%)
    pallas_call x1, Pallas kernels, local_block(): pl.pallas_call(functools.partial(block_kernel, chips), out_shape=pltpu.VM...  73.9 us

profile of v5, /device:TPU:81, one launch (start us, length us, event | category | flops | bytes accessed | tf_op | source)
XLA Modules:
  0.0 75.4 jit_solution(16275585553562398715)
XLA Ops:
  0.0 73.9 %gmlp_block.1 = bf16[4,256,1280]{2,1,0:T(8,128)(2,1)S(1)} custom-call(bf16[4,256,1280]{2,1,0:T(8,128)(2,1)} %x_hbm.1, f32[1280]{0:T(1024)} %ln1s_1d.1, f32[1280]{0:T(1024)} %ln1b_1d.1, bf16[1280,5120]{1,0:T(8,128)(2,1)} %w_in_hbm.1, f32[5120]{0:T(1024)} %b_in_1d.1, f32[2560]{0:T(1024)} %ln2s_1d.1, f32[2560]{0:T(1024)} %ln2b_1d.1, ...), custom_call_target="tpu_custom_call" | custom-call | tf_op jit(solution)/shard_map/gmlp_block/pallas_call | solution.py:330
  73.9 1.5 %copy.14 = bf16[4,256,1280]{2,1,0:T(8,128)(2,1)} copy(bf16[4,256,1280]{2,1,0:T(8,128)(2,1)S(1)} %gmlp_block.1) | data formatting | bytes 5242880

commit v6 on v5

--- a/solution.py
+++ b/solution.py
@@ -203,19 +203,19 @@
         half(g.at[j], 0, 0, 5)
         vn_copy(j).start()
 
+        @pl.when(h == 1)
+        def _():
+            xs_copy.wait()
+
+        @pl.when(h > 0)
+        def _():
+            start_sends(h + 1, xs)
+
+        half(g.at[j], 0, 5, gate // HT)
+
         @pl.when(h == 0)
         def _():
             start_sends(1, x_hbm)
-
-        @pl.when(h == 1)
-        def _():
-            xs_copy.wait()
-
-        @pl.when(h > 0)
-        def _():
-            start_sends(h + 1, xs)
-
-        half(g.at[j], 0, 5, gate // HT)
 
     def mask_weights():
         for cp in wm_copies + mk_copies:

time: 75.5 us -> 74.2 us (0.983)
  Pallas kernels: 73.9 us -> 72.5 us
    pallas_call x1, Pallas kernels: 73.9 us -> 72.5 us  [local_block(): pl.pallas_call(functools.partial(block_kernel, chips), out_shape=pltpu.VM...]
where the time goes in v6:
time: 74.2 us; the launch traced here: 74 us
  Pallas kernels  72.5 us (98%)
  local copies, waits for them, and re-layouts  1.49 us (2%)
    pallas_call x1, Pallas kernels, local_block(): pl.pallas_call(functools.partial(block_kernel, chips), out_shape=pltpu.VM...  72.5 us
    unnamed x1, local copies, waits for them, and re-layouts  1.49 us

profile of v6, /device:TPU:81, one launch (start us, length us, event | category | flops | bytes accessed | tf_op | source)
XLA Modules:
  0.0 74.0 jit_solution(10729243906473202606)
XLA Ops:
  0.0 72.5 %gmlp_block.1 = bf16[4,256,1280]{2,1,0:T(8,128)(2,1)S(1)} custom-call(bf16[4,256,1280]{2,1,0:T(8,128)(2,1)} %x_hbm.1, f32[1280]{0:T(1024)} %ln1s_1d.1, f32[1280]{0:T(1024)} %ln1b_1d.1, bf16[1280,5120]{1,0:T(8,128)(2,1)} %w_in_hbm.1, f32[5120]{0:T(1024)} %b_in_1d.1, f32[2560]{0:T(1024)} %ln2s_1d.1, f32[2560]{0:T(1024)} %ln2b_1d.1, ...), custom_call_target="tpu_custom_call" | custom-call | tf_op jit(solution)/shard_map/gmlp_block/pallas_call | solution.py:330
  72.6 1.5 %copy.14 = bf16[4,256,1280]{2,1,0:T(8,128)(2,1)} copy(bf16[4,256,1280]{2,1,0:T(8,128)(2,1)S(1)} %gmlp_block.1) | data formatting | bytes 5242880
